TPU v7x, 32 devices: a whole 2x2x4 slice. The times are simulated.
32 devices in a mesh: rep: 16 (over z, x, core), slab: 2 (over y).
Axes of the slice: x: 2, y: 2, z: 4, core: 2. Of those that a mesh axis runs over, the one named last changes fastest.
Arguments:
- weights: bfloat16 [16, 256, 3072], P('rep', 'slab'), may hold values from -6 to 6
- perms: int32 [16, 8, 256], P('rep'), may hold values from 0 to 255, each once within a row
Outputs:
- merged: bfloat16 [16, 256, 3072], P('rep', 'slab')
Inputs may be any that keep to these rules, and one draw needn't show every extreme that they name: `perms`: each row of 256 entries names every neuron of the window once.
All inputs are finite; a program needn't handle non-finite values.
Results may differ from a plain program's by a relative error of at most 0.012.
Values may be sent and summed in bfloat16 or wider, within the bound.
A program may use at most 64 MiB of HBM per device.

v0:
```python
import math

import jax
import jax.numpy as jnp
from jax import lax
from jax.sharding import PartitionSpec as P

D = 3072
ROUNDS = 8


def from_partner(x, axis, stride):
    return lax.ppermute(x, axis, [(i, i ^ 1 << stride) for i in range(lax.axis_size(axis))])


def finish_round(own, partner, perm_rows, cost):
    squared = cost * cost
    fourth = squared * squared
    soft_plan = fourth / (1.0 + jnp.sum(fourth, axis=1, keepdims=True))
    columns = jnp.arange(partner.shape[0], dtype=jnp.int32)
    onehot = (perm_rows[:, None] == columns[None, :]).astype(jnp.float32)
    mixing = (onehot + soft_plan).astype(jnp.bfloat16)
    aligned = 0.5 * jnp.dot(mixing, partner, preferred_element_type=jnp.float32)
    return ((own.astype(jnp.float32) + aligned) * (1.0 / math.sqrt(2.0))).astype(jnp.bfloat16)


def local(weights, perms):
    bit_count = lax.axis_size("rep").bit_length() - 1
    current = weights[0]
    perm_plan = perms[0]
    feature_part = lax.all_to_all(current, "slab", split_axis=1, concat_axis=0, tiled=True)
    for round_idx in range(ROUNDS):
        partner = from_partner(feature_part, "rep", round_idx % bit_count)
        partial_value = jnp.dot(feature_part, partner.T, preferred_element_type=jnp.float32)
        cost = lax.psum(partial_value, "slab") * (1.0 / math.sqrt(D))
        feature_part = finish_round(feature_part, partner, perm_plan[round_idx], cost)
    result = lax.all_to_all(feature_part, "slab", split_axis=0, concat_axis=1, tiled=True)
    return result[None]


def solution(mesh):
    placed = (P("rep", "slab", None), P("rep", None, None))
    return jax.shard_map(
        local, mesh=mesh, in_specs=placed, out_specs=P("rep", "slab", None), check_vma=False
    )
```

profile of v0, /device:TPU:7, one launch (start us, length us, event | category | flops | bytes accessed | tf_op | source)
XLA Modules:
  0.0 412.5 jit_solution(1840238187815374392)
XLA Ops:
  6.5 2.6 all_to_all.26
  9.2 11.6 %all_to_all.35 = bf16[128,2,1536]{2,0,1:T(8,128)(2,1)S(1)} all-to-all(bf16[128,2,1536]{2,0,1:T(8,128)(2,1)S(1)} %copy.3), channel_id=1, replica_groups=mesh['rep'=16,'slab'=2] {'slab'}, dimensions={1} | all-to-all | bytes 1572864 | tf_op jit(solution)/shard_map/all_to_all | solution.py:31
  22.1 1.9 collective-permute-done
  25.3 23.1 %all-reduce.9.cloned.1.call-done = f32[256,256]{1,0:T(8,128)} async-done(((f32[256,256]{1,0:T(8,128)}), f32[256,256]{1,0:T(8,128)}) %all-reduce.9.cloned.1.call-update) | async-done | bytes 262160 | tf_op jit(solution)/shard_map/psum | solution.py:35
  51.4 17.4 %collective-permute-done.1 = bf16[256,1536]{1,0:T(8,128)(2,1)S(1)} collective-permute-done((bf16[256,1536]{1,0:T(8,128)(2,1)S(1)}, bf16[256,1536]{1,0:T(8,128)(2,1)S(1)}, u32[]{:S(2)}, u32[]{:S(2)}) %collective-permute-start.1) | collective-permute-done | bytes 786464 | tf_op jit(solution)/shard_map/ppermute | solution.py:13
  70.0 24.3 %all-reduce.11.cloned.1.call-done = f32[256,256]{1,0:T(8,128)} async-done(((f32[256,256]{1,0:T(8,128)}), f32[256,256]{1,0:T(8,128)}) %all-reduce.11.cloned.1.call-update) | async-done | bytes 262160 | tf_op jit(solution)/shard_map/psum | solution.py:35
  98.0 16.7 %collective-permute-done.2 = bf16[256,1536]{1,0:T(8,128)(2,1)S(1)} collective-permute-done((bf16[256,1536]{1,0:T(8,128)(2,1)S(1)}, bf16[256,1536]{1,0:T(8,128)(2,1)S(1)}, u32[]{:S(2)}, u32[]{:S(2)}) %collective-permute-start.2) | collective-permute-done | bytes 786464 | tf_op jit(solution)/shard_map/ppermute | solution.py:13
  115.9 24.3 %all-reduce.13.cloned.1.call-done = f32[256,256]{1,0:T(8,128)} async-done(((f32[256,256]{1,0:T(8,128)}), f32[256,256]{1,0:T(8,128)}) %all-reduce.13.cloned.1.call-update) | async-done | bytes 262160 | tf_op jit(solution)/shard_map/psum | solution.py:35
  142.7 2.2 collective-permute-start.3
  144.9 34.2 %collective-permute-done.3 = bf16[256,1536]{1,0:T(8,128)(2,1)S(1)} collective-permute-done((bf16[256,1536]{1,0:T(8,128)(2,1)S(1)}, bf16[256,1536]{1,0:T(8,128)(2,1)S(1)}, u32[]{:S(2)}, u32[]{:S(2)}) %collective-permute-start.3) | collective-permute-done | bytes 786464 | tf_op jit(solution)/shard_map/ppermute | solution.py:13
  180.2 23.6 %all-reduce.15.cloned.1.call-done = f32[256,256]{1,0:T(8,128)} async-done(((f32[256,256]{1,0:T(8,128)}), f32[256,256]{1,0:T(8,128)}) %all-reduce.15.cloned.1.call-update) | async-done | bytes 262160 | tf_op jit(solution)/shard_map/psum | solution.py:35
  207.6 1.9 collective-permute-done.4
  210.7 22.6 %all-reduce.17.cloned.1.call-done = f32[256,256]{1,0:T(8,128)} async-done(((f32[256,256]{1,0:T(8,128)}), f32[256,256]{1,0:T(8,128)}) %all-reduce.17.cloned.1.call-update) | async-done | bytes 262160 | tf_op jit(solution)/shard_map/psum | solution.py:35
  236.4 17.4 %collective-permute-done.5 = bf16[256,1536]{1,0:T(8,128)(2,1)S(1)} collective-permute-done((bf16[256,1536]{1,0:T(8,128)(2,1)S(1)}, bf16[256,1536]{1,0:T(8,128)(2,1)S(1)}, u32[]{:S(2)}, u32[]{:S(2)}) %collective-permute-start.5) | collective-permute-done | bytes 786464 | tf_op jit(solution)/shard_map/ppermute | solution.py:13
  254.9 24.3 %all-reduce.19.cloned.1.call-done = f32[256,256]{1,0:T(8,128)} async-done(((f32[256,256]{1,0:T(8,128)}), f32[256,256]{1,0:T(8,128)}) %all-reduce.19.cloned.1.call-update) | async-done | bytes 262160 | tf_op jit(solution)/shard_map/psum | solution.py:35
  280.3 1.4 fusion.21
  283.0 16.7 %collective-permute-done.6 = bf16[256,1536]{1,0:T(8,128)(2,1)S(1)} collective-permute-done((bf16[256,1536]{1,0:T(8,128)(2,1)S(1)}, bf16[256,1536]{1,0:T(8,128)(2,1)S(1)}, u32[]{:S(2)}, u32[]{:S(2)}) %collective-permute-start.6) | collective-permute-done | bytes 786464 | tf_op jit(solution)/shard_map/ppermute | solution.py:13
  300.8 24.3 %all-reduce.21.cloned.1.call-done = f32[256,256]{1,0:T(8,128)} async-done(((f32[256,256]{1,0:T(8,128)}), f32[256,256]{1,0:T(8,128)}) %all-reduce.21.cloned.1.call-update) | async-done | bytes 262160 | tf_op jit(solution)/shard_map/psum | solution.py:35
  326.2 1.4 fusion.22
  327.6 2.2 collective-permute-start.7
  329.8 34.2 %collective-permute-done.7 = bf16[256,1536]{1,0:T(8,128)(2,1)S(1)} collective-permute-done((bf16[256,1536]{1,0:T(8,128)(2,1)S(1)}, bf16[256,1536]{1,0:T(8,128)(2,1)S(1)}, u32[]{:S(2)}, u32[]{:S(2)}) %collective-permute-start.7) | collective-permute-done | bytes 786464 | tf_op jit(solution)/shard_map/ppermute | solution.py:13
  365.1 23.7 %all-reduce.23.cloned.1.call-done = f32[256,256]{1,0:T(8,128)} async-done(((f32[256,256]{1,0:T(8,128)}), f32[256,256]{1,0:T(8,128)}) %all-reduce.23.cloned.1.call-update) | async-done | bytes 262160 | tf_op jit(solution)/shard_map/psum | solution.py:35
  391.3 12.1 %all_to_all.36 = bf16[2,128,1536]{2,1,0:T(8,128)(2,1)S(1)} all-to-all(bf16[2,128,1536]{2,1,0:T(8,128)(2,1)S(1)} %bitcast.41), channel_id=1, replica_groups=mesh['rep'=16,'slab'=2] {'slab'}, dimensions={0} | all-to-all | bytes 1572864 | tf_op jit(solution)/shard_map/all_to_all | solution.py:37
  404.2 1.5 broadcast_in_dim.2
  (57 shorter events, 33.5 us)
Async XLA Ops:
  6.5 41.8 %all-reduce.9.cloned.1.call-start = ((), (), s32[]{:S(2)}) async-start(), calls=%async_computation.2 | async-start | bytes 524288 | tf_op jit(solution)/shard_map/psum | solution.py:35
  20.7 4.5 %copy-start = (s32[1,8,256]{2,1,0:T(8,128)S(1)}, s32[1,8,256]{2,1,0:T(8,128)}, u32[]{:S(2)}) copy-start(s32[1,8,256]{2,1,0:T(8,128)} %param.3) | copy-start | bytes 24580
  20.8 3.3 collective-permute-start
  25.2 69.1 %all-reduce.11.cloned.1.call-start = ((), (), s32[]{:S(2)}) async-start(), calls=%async_computation.3 | async-start | bytes 524288 | tf_op jit(solution)/shard_map/psum | solution.py:35
  50.9 18.0 %collective-permute-start.1 = (bf16[256,1536]{1,0:T(8,128)(2,1)S(1)}, bf16[256,1536]{1,0:T(8,128)(2,1)S(1)}, u32[]{:S(2)}, u32[]{:S(2)}) collective-permute-start(bf16[256,1536]{1,0:T(8,128)(2,1)S(1)} %fusion.16), channel_id=1, source_target_pairs={{0,4},{2,6},{4,0},{6,2},{8,12},{10,14},{12,8},{14,10},{16,20},{18,... | collective-permute-start | bytes 2359304 | tf_op jit(solution)/shard_map/ppermute | solution.py:13
  70.0 70.2 %all-reduce.13.cloned.1.call-start = ((), (), s32[]{:S(2)}) async-start(), calls=%async_computation.4 | async-start | bytes 524288 | tf_op jit(solution)/shard_map/psum | solution.py:35
  96.8 18.0 %collective-permute-start.2 = (bf16[256,1536]{1,0:T(8,128)(2,1)S(1)}, bf16[256,1536]{1,0:T(8,128)(2,1)S(1)}, u32[]{:S(2)}, u32[]{:S(2)}) collective-permute-start(bf16[256,1536]{1,0:T(8,128)(2,1)S(1)} %fusion.17), channel_id=1, source_target_pairs={{0,8},{2,10},{4,12},{6,14},{8,0},{10,2},{12,4},{14,6},{16,24},{18,... | collective-permute-start | bytes 2359304 | tf_op jit(solution)/shard_map/ppermute | solution.py:13
  115.9 88.0 %all-reduce.15.cloned.1.call-start = ((), (), s32[]{:S(2)}) async-start(), calls=%async_computation.5 | async-start | bytes 524288 | tf_op jit(solution)/shard_map/psum | solution.py:35
  142.7 36.4 %collective-permute-start.3 = (bf16[256,1536]{1,0:T(8,128)(2,1)S(1)}, bf16[256,1536]{1,0:T(8,128)(2,1)S(1)}, u32[]{:S(2)}, u32[]{:S(2)}) collective-permute-start(bf16[256,1536]{1,0:T(8,128)(2,1)S(1)} %fusion.18), channel_id=1, source_target_pairs={{0,16},{2,18},{4,20},{6,22},{8,24},{10,26},{12,28},{14,30},{16,0},... | collective-permute-start | bytes 2359304 | tf_op jit(solution)/shard_map/ppermute | solution.py:13
  180.2 53.1 %all-reduce.17.cloned.1.call-start = ((), (), s32[]{:S(2)}) async-start(), calls=%async_computation.6 | async-start | bytes 524288 | tf_op jit(solution)/shard_map/psum | solution.py:35
  206.3 3.2 collective-permute-start.4
  210.6 68.6 %all-reduce.19.cloned.1.call-start = ((), (), s32[]{:S(2)}) async-start(), calls=%async_computation.7 | async-start | bytes 524288 | tf_op jit(solution)/shard_map/psum | solution.py:35
  235.8 18.0 %collective-permute-start.5 = (bf16[256,1536]{1,0:T(8,128)(2,1)S(1)}, bf16[256,1536]{1,0:T(8,128)(2,1)S(1)}, u32[]{:S(2)}, u32[]{:S(2)}) collective-permute-start(bf16[256,1536]{1,0:T(8,128)(2,1)S(1)} %fusion.20), channel_id=1, source_target_pairs={{0,4},{2,6},{4,0},{6,2},{8,12},{10,14},{12,8},{14,10},{16,20},{18,... | collective-permute-start | bytes 2359304 | tf_op jit(solution)/shard_map/ppermute | solution.py:13
  254.9 70.2 %all-reduce.21.cloned.1.call-start = ((), (), s32[]{:S(2)}) async-start(), calls=%async_computation.8 | async-start | bytes 524288 | tf_op jit(solution)/shard_map/psum | solution.py:35
  281.7 18.0 %collective-permute-start.6 = (bf16[256,1536]{1,0:T(8,128)(2,1)S(1)}, bf16[256,1536]{1,0:T(8,128)(2,1)S(1)}, u32[]{:S(2)}, u32[]{:S(2)}) collective-permute-start(bf16[256,1536]{1,0:T(8,128)(2,1)S(1)} %fusion.21), channel_id=1, source_target_pairs={{0,8},{2,10},{4,12},{6,14},{8,0},{10,2},{12,4},{14,6},{16,24},{18,... | collective-permute-start | bytes 2359304 | tf_op jit(solution)/shard_map/ppermute | solution.py:13
  300.8 88.0 %all-reduce.23.cloned.1.call-start = ((), (), s32[]{:S(2)}) async-start(), calls=%async_computation.9 | async-start | bytes 524288 | tf_op jit(solution)/shard_map/psum | solution.py:35
  327.6 36.4 %collective-permute-start.7 = (bf16[256,1536]{1,0:T(8,128)(2,1)S(1)}, bf16[256,1536]{1,0:T(8,128)(2,1)S(1)}, u32[]{:S(2)}, u32[]{:S(2)}) collective-permute-start(bf16[256,1536]{1,0:T(8,128)(2,1)S(1)} %fusion.22), channel_id=1, source_target_pairs={{0,16},{2,18},{4,20},{6,22},{8,24},{10,26},{12,28},{14,30},{16,0},... | collective-permute-start | bytes 2359304 | tf_op jit(solution)/shard_map/ppermute | solution.py:13
Sparse Core Ops, SparseCore 0:
  25.3 23.0 all-reduce.8
  70.1 24.1 all-reduce.10
  116.0 24.1 all-reduce.12
  180.3 23.5 all-reduce.14
  210.7 22.4 all-reduce.16
  255.0 24.1 all-reduce.18
  300.9 24.1 all-reduce.20
  365.2 23.5 all-reduce.22
where the time goes:
time: 417 us; the launch traced here: 413 us
  waiting for transfers between devices  330 us (79%)
  blocking collectives  23.7 us (6%)
  matrix products  20.1 us (5%)
  between operations  13.7 us (3%)
  starting transfers between devices  11.1 us (3%)
  other arithmetic  8.54 us (2%)
  local copies, waits for them, and re-layouts  4.93 us (1%)
    psum x8, waiting for transfers between devices, local(): cost = lax.psum(partial_value, 'slab') * (1.0 / math.sqrt(D))  190 us
    ppermute x8, waiting for transfers between devices, from_partner(): lax.ppermute(x, axis, [(i, i ^ 1 << stride) for i in range(lax.axis_size(...  140 us
    all_to_all x1, blocking collectives, local(): lax.all_to_all(feature_part, 'slab', split_axis=0, concat_axis=1, tiled=T...  12.1 us
    all_to_all x1, blocking collectives, local(): lax.all_to_all(current, 'slab', split_axis=1, concat_axis=0, tiled=True)  11.6 us
    dot_general x8, matrix products, finish_round(): aligned = 0.5 * jnp.dot(mixing, partner, preferred_element_type=jnp.float32)  11.3 us
    ppermute x8, starting transfers between devices, from_partner(): lax.ppermute(x, axis, [(i, i ^ 1 << stride) for i in range(lax.axis_size(...  10.8 us
    dot_general x8, matrix products, local(): jnp.dot(feature_part, partner.T, preferred_element_type=jnp.float32)  8.84 us
    reduce_sum x8, other arithmetic, finish_round(): soft_plan = fourth / (1.0 + jnp.sum(fourth, axis=1, keepdims=True))  8.51 us
  transfers between devices with their start and end apart: 16, of which 16 were waited for; matrix products, arithmetic and copies ran while one was open for 0% of the time, Pallas kernels for 0%

commit v1 on v0

v1 whole, which is shorter than its diff:
```python
import functools
import math

import jax
import jax.numpy as jnp
from jax import lax
from jax.experimental import pallas as pl
from jax.experimental.pallas import tpu as pltpu
from jax.sharding import PartitionSpec as P

CHUNK = 256


def placements(bits, rounds):
    position = {b: b for b in range(1, bits)}
    plan = [(0, None, dict(position))]
    for r in range(1, rounds):
        old, new = (r - 1) % bits, r % bits
        device_bit = position.pop(new)
        position[old] = device_bit
        plan.append((new, device_bit, dict(position)))
    return plan


def kernel(n_rep, n_slab, rounds, w_ref, p_ref, out_ref,
           state, sent, kept, part, core_in, slab_out, slab_in, cost_ref, perms,
           in_send, in_recv, ex_send, ex_recv, core_send, core_recv, slab_send, slab_recv,
           cost_send, cost_recv, out_send, out_recv, perm_send, perm_recv):
    bits = n_rep.bit_length() - 1
    me = lax.axis_index("rep")
    slab = lax.axis_index("slab")
    core = me % 2
    half, width = w_ref.shape[1], w_ref.shape[2]
    ffw = half * n_slab
    block = width // (2 * n_slab)
    chunks = block // CHUNK
    plan = placements(bits, rounds)

    def bit(b):
        return (me // (1 << b)) % 2

    def flipped(b):
        return me + (1 - 2 * bit(b)) * (1 << b)

    def remote(src, dst, send, recv, rep_to, slab_to):
        return pltpu.make_async_remote_copy(
            src_ref=src, dst_ref=dst, send_sem=send, recv_sem=recv,
            device_id=(rep_to, slab_to), device_id_type=pl.DeviceIdType.MESH)

    first_waits = []
    rows_here = pl.ds(pl.multiple_of(slab * half, half), half)
    for k in range(chunks):
        for ds_ in range(n_slab):
            for dc in range(2):
                rep_to = me if dc == 0 else flipped(0)
                core_to = core if dc == 0 else 1 - core
                slab_to = (slab + ds_) % n_slab
                start = (slab_to * 2 + core_to) * block + k * CHUNK
                src = w_ref.at[0, :, pl.ds(pl.multiple_of(start, CHUNK), CHUNK)]
                dst = state.at[core, k, rows_here]
                if ds_ == 0 and dc == 0:
                    copy = pltpu.make_async_copy(src, dst, in_recv.at[0, 0, k])
                else:
                    copy = remote(src, dst, in_send.at[ds_, dc, k], in_recv.at[ds_, dc, k], rep_to, slab_to)
                copy.start()
                first_waits.append((k, copy))

    perms[me] = p_ref[0]

    def spread(k, carry):
        to = lax.rem(me + k, n_rep)
        remote(p_ref.at[0], perms.at[me], perm_send, perm_recv, to, slab).start()
        return carry

    lax.fori_loop(1, n_rep, spread, 0)
    others = perms.at[pl.ds(0, n_rep - 1)]
    spread_all = remote(others, others, perm_send, perm_recv, flipped(0), slab)

    def contribution(a, b):
        return lax.dot_general(a, b, (((1,), (1,)), ((), ())), preferred_element_type=jnp.float32)

    pending = []
    exchange = None
    for r in range(rounds):
        local_bit, device_bit, position = plan[r]
        last = r == rounds - 1

        mine = None if device_bit is None else bit(device_bit)
        stays = mine if last else bit(plan[r + 1][1])
        if r == 0:
            first, second = 1 - stays, stays
        else:
            same = 1 - (stays + mine) % 2 if not last else 1
            first, second = 2 * r + same, 2 * r + 1 - same
        base = 0
        for b, p in position.items():
            base = base + bit(p) * (1 << b)
        first_rep = base + (1 - stays) * (1 << local_bit)
        second_rep = base + stays * (1 << local_bit)

        partial = None
        for k in range(chunks):
            if r == 0:
                for at, copy in first_waits:
                    if at == k:
                        copy.wait()
            else:
                exchange[k].wait_recv()
            term = contribution(state[first, k], state[second, k])
            partial = term if partial is None else partial + term
        part[r] = partial.reshape(2, ffw // 2, ffw)
        to_core = remote(part.at[r, 1 - core], core_in.at[r], core_send.at[r], core_recv.at[r], flipped(0), slab)
        to_core.start()
        if r == 0:
            spread_all.wait()
        columns = lax.broadcasted_iota(jnp.int32, (ffw, ffw), 1)
        rows = lax.broadcasted_iota(jnp.int32, (ffw, ffw), 0)
        first_perm = perms[first_rep].astype(jnp.float32).T[:, r:r + 1].astype(jnp.int32)
        second_perm = perms[second_rep, r:r + 1, :]
        first_hot = (first_perm == columns).astype(jnp.float32)
        second_hot = (second_perm == rows).astype(jnp.float32)
        to_core.wait_recv()
        total = part[r, core] + core_in[r]
        slab_out[r] = total.astype(slab_out.dtype)
        to_slabs = []
        for ds_ in range(1, n_slab):
            copy = remote(slab_out.at[r], slab_in.at[r, ds_ - 1], slab_send.at[r, ds_ - 1],
                          slab_recv.at[r, ds_ - 1], me, (slab + ds_) % n_slab)
            copy.start()
            to_slabs.append(copy)
        for ds_ in range(1, n_slab):
            to_slabs[ds_ - 1].wait_recv()
            total = total + slab_in[r, ds_ - 1].astype(jnp.float32)
        cost_ref[r, core] = total
        to_cost = remote(cost_ref.at[r, core], cost_ref.at[r, core], cost_send.at[r], cost_recv.at[r],
                         flipped(0), slab)
        to_cost.start()
        to_cost.wait_recv()
        pending += [to_core, to_cost] + to_slabs

        cost = cost_ref[r].reshape(ffw, ffw) * (1.0 / math.sqrt(width))
        squared = cost * cost
        fourth = squared * squared
        by_row = 1.0 / (1.0 + jnp.sum(fourth, axis=1, keepdims=True))
        by_column = 1.0 / (1.0 + jnp.sum(fourth, axis=0, keepdims=True))
        first_mix = (first_hot + fourth * by_row).astype(jnp.bfloat16)
        second_mix = (second_hot + fourth * by_column).T.astype(jnp.bfloat16)

        def merged(own, mix, other):
            aligned = 0.5 * jnp.dot(mix, other, preferred_element_type=jnp.float32)
            return ((own.astype(jnp.float32) + aligned) * (1.0 / math.sqrt(2.0))).astype(jnp.bfloat16)

        if not last:
            to = flipped(plan[r + 1][1])
            exchange = []
            for k in range(chunks):
                sent[r, k] = merged(state[first, k], first_mix, state[second, k])
                copy = remote(sent.at[r, k], state.at[2 * (r + 1) + 1, k], ex_send.at[r, k], ex_recv.at[r, k], to, slab)
                copy.start()
                exchange.append(copy)
            for k in range(chunks):
                state[2 * (r + 1), k] = merged(state[second, k], second_mix, state[first, k])
            pending += exchange
        else:
            source = slab * 2 + core

            def deliver(buffer, at, owner, k):
                for h in range(n_slab):
                    column = source * block + k * CHUNK
                    src = buffer.at[k, pl.ds(h * half, half)]
                    dst = out_ref.at[0, :, pl.ds(pl.multiple_of(column, CHUNK), CHUNK)]
                    stay = jnp.logical_and(owner == me, slab == h)

                    @pl.when(stay)
                    def _():
                        pltpu.make_async_copy(src, dst, out_recv.at[source, k]).start()

                    @pl.when(jnp.logical_not(stay))
                    def _():
                        remote(src, dst, out_send.at[at, h, k], out_recv.at[source, k], owner, h).start()

            for k in range(chunks):
                sent[r, k] = merged(state[first, k], first_mix, state[second, k])
                deliver(sent.at[r], 0, first_rep, k)
                kept[k] = merged(state[second, k], second_mix, state[first, k])
                deliver(kept, 1, second_rep, k)
            for k in range(chunks):
                for s in range(2 * n_slab):
                    dst = out_ref.at[0, :, pl.ds(s * block + k * CHUNK, CHUNK)]
                    pltpu.make_async_copy(dst, dst, out_recv.at[s, k]).wait()
                for at, owner, buffer in ((0, first_rep, sent.at[r]), (1, second_rep, kept)):
                    for h in range(n_slab):
                        @pl.when(jnp.logical_not(jnp.logical_and(owner == me, slab == h)))
                        def _():
                            src = buffer.at[k, pl.ds(h * half, half)]
                            dst = out_ref.at[0, :, pl.ds(k * CHUNK, CHUNK)]
                            remote(src, dst, out_send.at[at, h, k], out_recv.at[0, k], owner, h).wait_send()
    for copy in pending:
        copy.wait_send()


def solution(mesh):
    n_rep, n_slab = mesh.shape["rep"], mesh.shape["slab"]

    def local(weights, perms):
        _, half, width = weights.shape
        rounds = perms.shape[1]
        ffw = perms.shape[2]
        chunks = width // (2 * n_slab) // CHUNK
        vmem = pltpu.VMEM
        dma = pltpu.SemaphoreType.DMA
        bf16, f32 = jnp.bfloat16, jnp.float32
        return pl.pallas_call(
            functools.partial(kernel, n_rep, n_slab, rounds),
            out_shape=jax.ShapeDtypeStruct(weights.shape, weights.dtype),
            in_specs=[pl.BlockSpec(memory_space=pltpu.VMEM)] * 2,
            out_specs=pl.BlockSpec(memory_space=pltpu.VMEM),
            scratch_shapes=[
                vmem((2 * rounds, chunks, ffw, CHUNK), bf16),
                vmem((rounds, chunks, ffw, CHUNK), bf16),
                vmem((chunks, ffw, CHUNK), bf16),
                vmem((rounds, 2, ffw // 2, ffw), f32),
                vmem((rounds, ffw // 2, ffw), f32),
                vmem((rounds, ffw // 2, ffw), bf16),
                vmem((rounds, n_slab - 1, ffw // 2, ffw), bf16),
                vmem((rounds, 2, ffw // 2, ffw), f32),
                vmem((n_rep, rounds, ffw), jnp.int32),
                dma((n_slab, 2, chunks)), dma((n_slab, 2, chunks)),
                dma((rounds, chunks)), dma((rounds, chunks)),
                dma((rounds,)), dma((rounds,)),
                dma((rounds, n_slab - 1)), dma((rounds, n_slab - 1)),
                dma((rounds,)), dma((rounds,)),
                dma((2, n_slab, chunks)), dma((2 * n_slab, chunks)),
                dma, dma,
            ],
            compiler_params=pltpu.CompilerParams(has_side_effects=True, vmem_limit_bytes=60 * 1024 * 1024),
        )(weights, perms)

    return jax.shard_map(
        local, mesh=mesh, in_specs=(P("rep", "slab", None), P("rep", None, None)),
        out_specs=P("rep", "slab", None), check_vma=False,
    )
```

time: 417 us -> 185 us (0.44); the launches traced: 413 us -> 185 us
  waiting for transfers between devices: 330 us -> 0 us
  Pallas kernels: 0 us -> 183 us
  blocking collectives: 23.7 us -> 0 us
  matrix products: 20.1 us -> 0 us
  between operations: 13.7 us -> 0.01 us
  starting transfers between devices: 11.1 us -> 0 us
  other arithmetic: 8.54 us -> 0 us
    psum x8 -> x0, waiting for transfers between devices: 190 us -> none  [local(): cost = lax.psum(partial_value, 'slab') * (1.0 / math.sqrt(D))]
    pallas_call x0 -> x1, Pallas kernels: none -> 183 us  [local(): pl.pallas_call(functools.partial(kernel, n_rep, n_slab, rounds), out_shap...]
    ppermute x8 -> x0, waiting for transfers between devices: 140 us -> none  [from_partner(): lax.ppermute(x, axis, [(i, i ^ 1 << stride) for i in range(lax.axis_size(...]
    all_to_all x2 -> x0, blocking collectives: 23.7 us -> none  [the longest x1 12.1 us: local(): lax.all_to_all(feature_part, 'slab', split_axis=0, concat_axis=1, tiled=T...]
    dot_general x16 -> x0, matrix products: 20.1 us -> none  [the longest x8 11.3 us: finish_round(): aligned = 0.5 * jnp.dot(mixing, partner, preferred_element_type=jnp.float32)]
    ppermute x8 -> x0, starting transfers between devices: 10.8 us -> none  [from_partner(): lax.ppermute(x, axis, [(i, i ^ 1 << stride) for i in range(lax.axis_size(...]
    reduce_sum x8 -> x0, other arithmetic: 8.51 us -> none  [finish_round(): soft_plan = fourth / (1.0 + jnp.sum(fourth, axis=1, keepdims=True))]
  transfers between devices with their start and end apart: 16 -> 0, of which waited for: 16 -> 0; matrix products, arithmetic and copies ran while one was open for 0% -> 0% of each run, Pallas kernels for 0% -> 0%
where the time goes in v1:
time: 185 us
  Pallas kernels  183 us (99%)
  local copies, waits for them, and re-layouts  2.06 us (1%)
    pallas_call x1, Pallas kernels, local(): pl.pallas_call(functools.partial(kernel, n_rep, n_slab, rounds), out_shap...  183 us

profile of v1, /device:TPU:7, one launch (start us, length us, event | category | flops | bytes accessed | tf_op | source)
XLA Modules:
  0.0 185.3 jit_solution(5332631517032838752)
XLA Ops:
  0.0 183.2 %shard_map.28 = bf16[1,128,3072]{2,1,0:T(8,128)(2,1)} custom-call(bf16[1,128,3072]{2,1,0:T(8,128)(2,1)} %w_ref.1, s32[1,8,256]{2,1,0:T(8,128)} %p_ref.1), custom_call_target="tpu_custom_call" | custom-call | tf_op jit(solution)/shard_map/pallas_call | solution.py:213
  183.2 2.1 %copy.4 = bf16[1,128,3072]{2,1,0:T(8,128)(2,1)} copy(bf16[1,128,3072]{2,1,0:T(8,128)(2,1)} %shard_map.28) | data formatting | bytes 1572864

commit v2 on v1

--- a/solution.py
+++ b/solution.py
@@ -23,7 +23,7 @@
 
 
 def kernel(n_rep, n_slab, rounds, w_ref, p_ref, out_ref,
-           state, sent, kept, part, core_in, slab_out, slab_in, cost_ref, perms,
+           state, sent, kept, part, core_in, slab_out, slab_in, cost_ref, perms, hot,
            in_send, in_recv, ex_send, ex_recv, core_send, core_recv, slab_send, slab_recv,
            cost_send, cost_recv, out_send, out_recv, perm_send, perm_recv):
     bits = n_rep.bit_length() - 1
@@ -105,7 +105,8 @@
                     if at == k:
                         copy.wait()
             else:
-                exchange[k].wait_recv()
+                exchange[0][k].wait_recv()
+                exchange[1][k].wait_recv()
             term = contribution(state[first, k], state[second, k])
             partial = term if partial is None else partial + term
         part[r] = partial.reshape(2, ffw // 2, ffw)
@@ -135,55 +136,76 @@
         to_cost = remote(cost_ref.at[r, core], cost_ref.at[r, core], cost_send.at[r], cost_recv.at[r],
                          flipped(0), slab)
         to_cost.start()
-        to_cost.wait_recv()
         pending += [to_core, to_cost] + to_slabs
 
-        cost = cost_ref[r].reshape(ffw, ffw) * (1.0 / math.sqrt(width))
-        squared = cost * cost
-        fourth = squared * squared
-        by_row = 1.0 / (1.0 + jnp.sum(fourth, axis=1, keepdims=True))
-        by_column = 1.0 / (1.0 + jnp.sum(fourth, axis=0, keepdims=True))
-        first_mix = (first_hot + fourth * by_row).astype(jnp.bfloat16)
-        second_mix = (second_hot + fourth * by_column).T.astype(jnp.bfloat16)
+        scale = 1.0 / math.sqrt(width)
+        mine_rows = pl.ds(pl.multiple_of(core * (ffw // 2), ffw // 2), ffw // 2)
+        other_rows = pl.ds(pl.multiple_of((1 - core) * (ffw // 2), ffw // 2), ffw // 2)
 
         def merged(own, mix, other):
             aligned = 0.5 * jnp.dot(mix, other, preferred_element_type=jnp.float32)
             return ((own.astype(jnp.float32) + aligned) * (1.0 / math.sqrt(2.0))).astype(jnp.bfloat16)
 
+        if last:
+            source = slab * 2 + core
+
+            def deliver(buffer, at, owner, h, k):
+                column = source * block + k * CHUNK
+                src = buffer.at[k, pl.ds(pl.multiple_of(h * half, half), half)]
+                dst = out_ref.at[0, :, pl.ds(pl.multiple_of(column, CHUNK), CHUNK)]
+                stay = jnp.logical_and(owner == me, slab == h)
+
+                @pl.when(stay)
+                def _():
+                    pltpu.make_async_copy(src, dst, out_recv.at[source, k]).start()
+
+                @pl.when(jnp.logical_not(stay))
+                def _():
+                    remote(src, dst, out_send.at[at, h, k], out_recv.at[source, k], owner, h).start()
+        else:
+            exchange = [[], []]
+
+        fourths = []
+        for part_at, its_rows in enumerate((mine_rows, other_rows)):
+            if part_at == 1:
+                to_cost.wait_recv()
+            cost = (total if part_at == 0 else cost_ref[r, 1 - core]) * scale
+            squared = cost * cost
+            fourth = squared * squared
+            fourths.append(fourth)
+            by_row = 1.0 / (1.0 + jnp.sum(fourth, axis=1, keepdims=True))
+            if part_at == 0:
+                hot[...] = first_hot
+            mix = (hot[its_rows, :] + fourth * by_row).astype(jnp.bfloat16)
+            for k in range(chunks):
+                sent[r, k, its_rows, :] = merged(state[first, k, its_rows, :], mix, state[second, k])
+                if not last:
+                    copy = remote(sent.at[r, k, its_rows], state.at[2 * (r + 1) + 1, k, its_rows],
+                                  ex_send.at[r, part_at, k], ex_recv.at[r, part_at, k],
+                                  flipped(plan[r + 1][1]), slab)
+                    copy.start()
+                    exchange[part_at].append(copy)
+                elif n_slab == 2:
+                    deliver(sent.at[r], 0, first_rep, core if part_at == 0 else 1 - core, k)
+            if last and n_slab != 2 and part_at == 1:
+                for k in range(chunks):
+                    for h in range(n_slab):
+                        deliver(sent.at[r], 0, first_rep, h, k)
+        by_column = 1.0 / (1.0 + sum(jnp.sum(f, axis=0, keepdims=True) for f in fourths))
+        for f, its_rows in zip(fourths, (mine_rows, other_rows)):
+            hot[its_rows, :] = f * by_column
+        second_mix = (second_hot + hot[...]).T.astype(jnp.bfloat16)
+        for k in range(chunks):
+            new = merged(state[second, k], second_mix, state[first, k])
+            if last:
+                kept[k] = new
+                for h in range(n_slab):
+                    deliver(kept, 1, second_rep, h, k)
+            else:
+                state[2 * (r + 1), k] = new
         if not last:
-            to = flipped(plan[r + 1][1])
-            exchange = []
-            for k in range(chunks):
-                sent[r, k] = merged(state[first, k], first_mix, state[second, k])
-                copy = remote(sent.at[r, k], state.at[2 * (r + 1) + 1, k], ex_send.at[r, k], ex_recv.at[r, k], to, slab)
-                copy.start()
-                exchange.append(copy)
-            for k in range(chunks):
-                state[2 * (r + 1), k] = merged(state[second, k], second_mix, state[first, k])
-            pending += exchange
+            pending += exchange[0] + exchange[1]
         else:
-            source = slab * 2 + core
-
-            def deliver(buffer, at, owner, k):
-                for h in range(n_slab):
-                    column = source * block + k * CHUNK
-                    src = buffer.at[k, pl.ds(h * half, half)]
-                    dst = out_ref.at[0, :, pl.ds(pl.multiple_of(column, CHUNK), CHUNK)]
-                    stay = jnp.logical_and(owner == me, slab == h)
-
-                    @pl.when(stay)
-                    def _():
-                        pltpu.make_async_copy(src, dst, out_recv.at[source, k]).start()
-
-                    @pl.when(jnp.logical_not(stay))
-                    def _():
-                        remote(src, dst, out_send.at[at, h, k], out_recv.at[source, k], owner, h).start()
-
-            for k in range(chunks):
-                sent[r, k] = merged(state[first, k], first_mix, state[second, k])
-                deliver(sent.at[r], 0, first_rep, k)
-                kept[k] = merged(state[second, k], second_mix, state[first, k])
-                deliver(kept, 1, second_rep, k)
             for k in range(chunks):
                 for s in range(2 * n_slab):
                     dst = out_ref.at[0, :, pl.ds(s * block + k * CHUNK, CHUNK)]
@@ -225,8 +247,9 @@
                 vmem((rounds, n_slab - 1, ffw // 2, ffw), bf16),
                 vmem((rounds, 2, ffw // 2, ffw), f32),
                 vmem((n_rep, rounds, ffw), jnp.int32),
+                vmem((ffw, ffw), f32),
                 dma((n_slab, 2, chunks)), dma((n_slab, 2, chunks)),
-                dma((rounds, chunks)), dma((rounds, chunks)),
+                dma((rounds, 2, chunks)), dma((rounds, 2, chunks)),
                 dma((rounds,)), dma((rounds,)),
                 dma((rounds, n_slab - 1)), dma((rounds, n_slab - 1)),
                 dma((rounds,)), dma((rounds,)),

time: 185 us -> 174 us (0.941)
  Pallas kernels: 183 us -> 171 us
    pallas_call x1, Pallas kernels: 183 us -> 171 us  [local(): pl.pallas_call(functools.partial(kernel, n_rep, n_slab, rounds), out_shap...]
where the time goes in v2:
time: 174 us; the launch traced here: 173 us
  Pallas kernels  171 us (98%)
  local copies, waits for them, and re-layouts  2.06 us (1%)
    pallas_call x1, Pallas kernels, local(): pl.pallas_call(functools.partial(kernel, n_rep, n_slab, rounds), out_shap...  171 us

profile of v2, /device:TPU:7, one launch (start us, length us, event | category | flops | bytes accessed | tf_op | source)
XLA Modules:
  0.0 173.4 jit_solution(12647765785848987332)
XLA Ops:
  0.0 171.4 %shard_map.28 = bf16[1,128,3072]{2,1,0:T(8,128)(2,1)} custom-call(bf16[1,128,3072]{2,1,0:T(8,128)(2,1)} %w_ref.1, s32[1,8,256]{2,1,0:T(8,128)} %p_ref.1), custom_call_target="tpu_custom_call" | custom-call | tf_op jit(solution)/shard_map/pallas_call | solution.py:235
  171.4 2.1 %copy.4 = bf16[1,128,3072]{2,1,0:T(8,128)(2,1)} copy(bf16[1,128,3072]{2,1,0:T(8,128)(2,1)} %shard_map.28) | data formatting | bytes 1572864

commit v3 on v2

--- a/solution.py
+++ b/solution.py
@@ -46,6 +46,18 @@
         return pltpu.make_async_remote_copy(
             src_ref=src, dst_ref=dst, send_sem=send, recv_sem=recv,
             device_id=(rep_to, slab_to), device_id_type=pl.DeviceIdType.MESH)
+
+    barrier = pltpu.get_barrier_semaphore()
+    devices = n_rep * n_slab
+
+    def greet(k, carry):
+        to = lax.rem(me * n_slab + slab + k, devices)
+        pl.semaphore_signal(barrier, inc=1, device_id=(to // n_slab, to % n_slab),
+                            device_id_type=pl.DeviceIdType.MESH)
+        return carry
+
+    lax.fori_loop(1, devices, greet, 0)
+    pl.semaphore_wait(barrier, devices - 1)
 
     first_waits = []
     rows_here = pl.ds(pl.multiple_of(slab * half, half), half)
@@ -256,7 +268,7 @@
                 dma((2, n_slab, chunks)), dma((2 * n_slab, chunks)),
                 dma, dma,
             ],
-            compiler_params=pltpu.CompilerParams(has_side_effects=True, vmem_limit_bytes=60 * 1024 * 1024),
+            compiler_params=pltpu.CompilerParams(collective_id=0, has_side_effects=True, vmem_limit_bytes=60 * 1024 * 1024),
         )(weights, perms)
 
     return jax.shard_map(

time: 174 us -> 170 us (0.977); the launches traced: 173 us -> 167 us
  Pallas kernels: 171 us -> 165 us
    pallas_call x1, Pallas kernels: 171 us -> 165 us  [local(): pl.pallas_call(functools.partial(kernel, n_rep, n_slab, rounds), out_shap...]
where the time goes in v3:
time: 170 us; the launch traced here: 167 us
  Pallas kernels  165 us (97%)
  local copies, waits for them, and re-layouts  2.06 us (1%)
    pallas_call x1, Pallas kernels, local(): pl.pallas_call(functools.partial(kernel, n_rep, n_slab, rounds), out_shap...  165 us

profile of v3, /device:TPU:7, one launch (start us, length us, event | category | flops | bytes accessed | tf_op | source)
XLA Modules:
  0.0 167.1 jit_solution(17517620418050490975)
XLA Ops:
  0.0 165.1 %shard_map.28 = bf16[1,128,3072]{2,1,0:T(8,128)(2,1)} custom-call(bf16[1,128,3072]{2,1,0:T(8,128)(2,1)} %w_ref.1, s32[1,8,256]{2,1,0:T(8,128)} %p_ref.1), custom_call_target="tpu_custom_call" | custom-call | tf_op jit(solution)/shard_map/pallas_call | solution.py:247
  165.1 2.1 %copy.4 = bf16[1,128,3072]{2,1,0:T(8,128)(2,1)} copy(bf16[1,128,3072]{2,1,0:T(8,128)(2,1)} %shard_map.28) | data formatting | bytes 1572864

commit v4 on v3

--- a/solution.py
+++ b/solution.py
@@ -9,6 +9,7 @@
 from jax.sharding import PartitionSpec as P
 
 CHUNK = 256
+PIECES = 2
 
 
 def placements(bits, rounds):
@@ -117,13 +118,19 @@
                     if at == k:
                         copy.wait()
             else:
-                exchange[0][k].wait_recv()
-                exchange[1][k].wait_recv()
+                for piece in exchange:
+                    piece[k].wait_recv()
             term = contribution(state[first, k], state[second, k])
             partial = term if partial is None else partial + term
         part[r] = partial.reshape(2, ffw // 2, ffw)
-        to_core = remote(part.at[r, 1 - core], core_in.at[r], core_send.at[r], core_recv.at[r], flipped(0), slab)
-        to_core.start()
+        quarter = ffw // 2 // PIECES
+        to_cores = []
+        for q in range(PIECES):
+            its = pl.ds(q * quarter, quarter)
+            copy = remote(part.at[r, 1 - core, its], core_in.at[r, its], core_send.at[r, q], core_recv.at[r, q],
+                          flipped(0), slab)
+            copy.start()
+            to_cores.append(copy)
         if r == 0:
             spread_all.wait()
         columns = lax.broadcasted_iota(jnp.int32, (ffw, ffw), 1)
@@ -132,27 +139,26 @@
         second_perm = perms[second_rep, r:r + 1, :]
         first_hot = (first_perm == columns).astype(jnp.float32)
         second_hot = (second_perm == rows).astype(jnp.float32)
-        to_core.wait_recv()
-        total = part[r, core] + core_in[r]
-        slab_out[r] = total.astype(slab_out.dtype)
         to_slabs = []
-        for ds_ in range(1, n_slab):
-            copy = remote(slab_out.at[r], slab_in.at[r, ds_ - 1], slab_send.at[r, ds_ - 1],
-                          slab_recv.at[r, ds_ - 1], me, (slab + ds_) % n_slab)
-            copy.start()
-            to_slabs.append(copy)
-        for ds_ in range(1, n_slab):
-            to_slabs[ds_ - 1].wait_recv()
-            total = total + slab_in[r, ds_ - 1].astype(jnp.float32)
-        cost_ref[r, core] = total
-        to_cost = remote(cost_ref.at[r, core], cost_ref.at[r, core], cost_send.at[r], cost_recv.at[r],
-                         flipped(0), slab)
-        to_cost.start()
-        pending += [to_core, to_cost] + to_slabs
+        for q in range(PIECES):
+            its = pl.ds(q * quarter, quarter)
+            to_cores[q].wait_recv()
+            total = part[r, core, its, :] + core_in[r, its, :]
+            cost_ref[r, core, its, :] = total
+            slab_out[r, its, :] = total.astype(slab_out.dtype)
+            for ds_ in range(1, n_slab):
+                copy = remote(slab_out.at[r, its], slab_in.at[r, ds_ - 1, its], slab_send.at[r, ds_ - 1, q],
+                              slab_recv.at[r, ds_ - 1, q], me, (slab + ds_) % n_slab)
+                copy.start()
+                to_slabs.append(copy)
+        to_costs = []
+        pending += to_cores + to_slabs
 
         scale = 1.0 / math.sqrt(width)
-        mine_rows = pl.ds(pl.multiple_of(core * (ffw // 2), ffw // 2), ffw // 2)
-        other_rows = pl.ds(pl.multiple_of((1 - core) * (ffw // 2), ffw // 2), ffw // 2)
+        half_rows = ffw // 2
+        row_sets = [pl.ds(pl.multiple_of(core * half_rows + q * quarter, quarter), quarter) for q in range(PIECES)]
+        row_sets += [pl.ds(pl.multiple_of((1 - core) * half_rows + q * quarter, quarter), quarter)
+                     for q in range(PIECES)]
 
         def merged(own, mix, other):
             aligned = 0.5 * jnp.dot(mix, other, preferred_element_type=jnp.float32)
@@ -175,13 +181,26 @@
                 def _():
                     remote(src, dst, out_send.at[at, h, k], out_recv.at[source, k], owner, h).start()
         else:
-            exchange = [[], []]
+            exchange = [[] for _ in row_sets]
 
         fourths = []
-        for part_at, its_rows in enumerate((mine_rows, other_rows)):
-            if part_at == 1:
-                to_cost.wait_recv()
-            cost = (total if part_at == 0 else cost_ref[r, 1 - core]) * scale
+        for part_at, its_rows in enumerate(row_sets):
+            q = part_at % PIECES
+            its = pl.ds(q * quarter, quarter)
+            if part_at < PIECES:
+                total = cost_ref[r, core, its, :]
+                for ds_ in range(1, n_slab):
+                    to_slabs[q * (n_slab - 1) + ds_ - 1].wait_recv()
+                    total = total + slab_in[r, ds_ - 1, its, :].astype(jnp.float32)
+                cost_ref[r, core, its, :] = total
+                copy = remote(cost_ref.at[r, core, its], cost_ref.at[r, core, its], cost_send.at[r, q],
+                              cost_recv.at[r, q], flipped(0), slab)
+                copy.start()
+                to_costs.append(copy)
+            else:
+                to_costs[q].wait_recv()
+                total = cost_ref[r, 1 - core, its, :]
+            cost = total * scale
             squared = cost * cost
             fourth = squared * squared
             fourths.append(fourth)
@@ -197,14 +216,14 @@
                                   flipped(plan[r + 1][1]), slab)
                     copy.start()
                     exchange[part_at].append(copy)
-                elif n_slab == 2:
-                    deliver(sent.at[r], 0, first_rep, core if part_at == 0 else 1 - core, k)
-            if last and n_slab != 2 and part_at == 1:
+                elif n_slab == 2 and q == PIECES - 1:
+                    deliver(sent.at[r], 0, first_rep, core if part_at < PIECES else 1 - core, k)
+            if last and n_slab != 2 and part_at == len(row_sets) - 1:
                 for k in range(chunks):
                     for h in range(n_slab):
                         deliver(sent.at[r], 0, first_rep, h, k)
         by_column = 1.0 / (1.0 + sum(jnp.sum(f, axis=0, keepdims=True) for f in fourths))
-        for f, its_rows in zip(fourths, (mine_rows, other_rows)):
+        for f, its_rows in zip(fourths, row_sets):
             hot[its_rows, :] = f * by_column
         second_mix = (second_hot + hot[...]).T.astype(jnp.bfloat16)
         for k in range(chunks):
@@ -216,8 +235,9 @@
             else:
                 state[2 * (r + 1), k] = new
         if not last:
-            pending += exchange[0] + exchange[1]
+            pending += sum(exchange, []) + to_costs
         else:
+            pending += to_costs
             for k in range(chunks):
                 for s in range(2 * n_slab):
                     dst = out_ref.at[0, :, pl.ds(s * block + k * CHUNK, CHUNK)]
@@ -261,10 +281,10 @@
                 vmem((n_rep, rounds, ffw), jnp.int32),
                 vmem((ffw, ffw), f32),
                 dma((n_slab, 2, chunks)), dma((n_slab, 2, chunks)),
-                dma((rounds, 2, chunks)), dma((rounds, 2, chunks)),
-                dma((rounds,)), dma((rounds,)),
-                dma((rounds, n_slab - 1)), dma((rounds, n_slab - 1)),
-                dma((rounds,)), dma((rounds,)),
+                dma((rounds, 2 * PIECES, chunks)), dma((rounds, 2 * PIECES, chunks)),
+                dma((rounds, PIECES)), dma((rounds, PIECES)),
+                dma((rounds, n_slab - 1, PIECES)), dma((rounds, n_slab - 1, PIECES)),
+                dma((rounds, PIECES)), dma((rounds, PIECES)),
                 dma((2, n_slab, chunks)), dma((2 * n_slab, chunks)),
                 dma, dma,
             ],

time: 170 us -> 168 us (0.988)
  Pallas kernels: 165 us -> 163 us
    pallas_call x1, Pallas kernels: 165 us -> 163 us  [local(): pl.pallas_call(functools.partial(kernel, n_rep, n_slab, rounds), out_shap...]
where the time goes in v4:
time: 168 us; the launch traced here: 165 us
  Pallas kernels  163 us (97%)
  local copies, waits for them, and re-layouts  2.06 us (1%)
    pallas_call x1, Pallas kernels, local(): pl.pallas_call(functools.partial(kernel, n_rep, n_slab, rounds), out_shap...  163 us

profile of v4, /device:TPU:7, one launch (start us, length us, event | category | flops | bytes accessed | tf_op | source)
XLA Modules:
  0.0 165.0 jit_solution(8494460703158365468)
XLA Ops:
  0.0 162.9 %shard_map.28 = bf16[1,128,3072]{2,1,0:T(8,128)(2,1)} custom-call(bf16[1,128,3072]{2,1,0:T(8,128)(2,1)} %w_ref.1, s32[1,8,256]{2,1,0:T(8,128)} %p_ref.1), custom_call_target="tpu_custom_call" | custom-call | tf_op jit(solution)/shard_map/pallas_call | solution.py:267
  162.9 2.1 %copy.4 = bf16[1,128,3072]{2,1,0:T(8,128)(2,1)} copy(bf16[1,128,3072]{2,1,0:T(8,128)(2,1)} %shard_map.28) | data formatting | bytes 1572864
